TPU v7x, 512 devices: a whole 4x8x8 slice. The times are simulated.
512 devices in a mesh: lat: 16 (over y_lo, z), lon: 32 (over y_hi, x, core).
Axes of the slice: x: 4, y: 8 (y_hi: 4, y_lo: 2; y = y_hi * 2 + y_lo), z: 8, core: 2. Of those that a mesh axis runs over, the one named last changes fastest.
Arguments:
- state_grid: bfloat16 [96, 2688, 192], P('lat', 'lon'), may hold values from -6 to 6
- norm_gain: float32 [192], replicated, may hold values from 0.1 to 1.9
- w_qkv: bfloat16 [192, 576], replicated, may hold values from -0.4375 to 0.4375
- w_proj: bfloat16 [192, 192], replicated, may hold values from -1.25 to 1.25
- bias_table: float32 [8, 6, 253], replicated, may hold values from -6 to 300
- window_kind: int32 [16, 224], replicated, may hold values from 0 to 7
- cotangent: bfloat16 [96, 2688, 192], P('lat', 'lon'), may hold values from -6 to 6
Outputs:
- out_field: bfloat16 [96, 2688, 192], P('lat', 'lon')
- d_field: bfloat16 [96, 2688, 192], P('lat', 'lon')
- qkv_grad: float32 [192, 576], replicated
- proj_grad: float32 [192, 192], replicated
- table_grad: float32 [8, 6, 253], replicated
- gain_grad: float32 [192], replicated
All inputs are finite; a program needn't handle non-finite values.
Results may differ from a plain program's by a relative error of at most 0.009.
Values may be sent and summed in bfloat16 or wider, within the bound.
No kernel may reach another device: no remote copies, remote signals or barrier semaphores. Data moves between devices by JAX's collectives and lax.ppermute only.
A program may use at most 64 MiB of HBM per device.

v0:
```python
import functools
import jax
import jax.numpy as jnp
from jax import lax
from jax.experimental import pallas as pl
from jax.experimental.pallas import tpu as pltpu
from jax.sharding import Mesh, PartitionSpec as P

HEADS = 6
WIN_LAT = 6
WIN_LON = 12
HEAD = 32
D = 192
PITCH = 16
TOK = WIN_LAT * PITCH
LANES = 128
SPAN = 256
norm_eps = 1e-05
clip_eps = 1e-06
masked = -1e30
AT_TABLE = 6 * D
AT_GAIN = AT_TABLE + 96
ROWS = 1280
VM_ATTEND = 28
VM_FINISH = 8
VM_BIAS = 10
VM_RESULTS = 8
LAT = ("y_lo", "z_hi", "z_lo")
LON = ("y_hi", "x", "core")
PARTS = (2, 4, 2, 4, 4, 2)
SLICED = ("y_lo", "z_lo", "x", "core")
WHOLE = ("z_hi", "y_hi")
highest = lax.Precision.HIGHEST
f32 = jnp.float32
bf16 = jnp.bfloat16

NT = (((1,), (1,)), ((), ()))
TN = (((0,), (0,)), ((), ()))


def nt(a, b, **kw):
    return lax.dot_general(a, b, NT, preferred_element_type=f32, **kw)


def tn(a, b, **kw):
    return lax.dot_general(a, b, TN, preferred_element_type=f32, **kw)


def nn(a, b, **kw):
    return jnp.dot(a, b, preferred_element_type=f32, **kw)


def iota(shape, dim):
    return lax.broadcasted_iota(jnp.int32, shape, dim)


def base_pattern():
    p = iota((SPAN, SPAN), 0)
    lane = iota((SPAN, SPAN), 1)
    d = lane // PITCH
    c = lane % PITCH
    hit = (p == (2 * WIN_LAT - 2 - d) * (2 * WIN_LON - 1) - c + WIN_LON - 1) & (c < WIN_LON) & (d < 2 * WIN_LAT - 1)
    return hit.astype(f32)


def bias_kernel(table_ref, last_ref, bias, tab, tilt, span):
    half_lat = WIN_LAT // 2
    kinds = table_ref.shape[0] // HEADS
    tab[...] = jnp.zeros_like(tab)
    tab[:, :table_ref.shape[1]] = table_ref[...]
    for c in range(PITCH):
        moved = tab[...] if c == 0 else pltpu.roll(tab[...], SPAN - c, axis=1)
        for half in range(2):
            tilt[half, pl.ds(c, kinds * HEADS, stride=PITCH), :] = moved[:, half * LANES:(half + 1) * LANES]
    pattern = base_pattern()
    span[...] = nn(jnp.concatenate([tilt[0], tilt[1]], axis=1), pattern, precision=highest)
    slot = iota((PITCH, LANES), 1)
    open_slot = (slot % PITCH < WIN_LON) & (slot < TOK)
    split = last_ref[0] > 0

    def spread(n, carry):
        wide = span[pl.ds(pl.multiple_of(n * PITCH, PITCH), PITCH), :]
        for r in range(WIN_LAT):
            off = (WIN_LAT - 1 - r) * PITCH
            part = wide if off == 0 else pltpu.roll(wide, SPAN - off, axis=1)
            other = (slot < half_lat * PITCH) if r >= half_lat else (slot >= half_lat * PITCH)
            ok = open_slot & jnp.logical_not(split & other)
            bias[n % kinds, pl.ds(pl.multiple_of((n // kinds) * TOK + r * PITCH, PITCH), PITCH), :] = jnp.where(ok, part[:, :LANES], masked)
        return carry

    lax.fori_loop(0, kinds * HEADS, spread, 0, unroll=True)


def bias_of(table, last):
    vm = pl.BlockSpec(memory_space=pltpu.VMEM)
    kh = table.shape[0]
    return pl.pallas_call(
        bias_kernel,
        out_shape=jax.ShapeDtypeStruct((kh // HEADS, HEADS * TOK, LANES), f32),
        in_specs=[vm, pl.BlockSpec(memory_space=pltpu.SMEM)],
        out_specs=vm,
        scratch_shapes=[
            pltpu.VMEM((kh, SPAN), f32), pltpu.VMEM((2, kh * PITCH, LANES), f32), pltpu.VMEM((kh * PITCH, SPAN), f32),
        ],
        cost_estimate=pl.CostEstimate(flops=600_000_000, bytes_accessed=2_500_000, transcendentals=0),
        compiler_params=pltpu.CompilerParams(vmem_limit_bytes=VM_BIAS << 20),
        name="bias",
    )(table, last)


def kernel(windows, kinds, meta_ref, own_ref, up_ref, side_ref, corner_ref, gain_ref, wqkv_ref, wproj_ref, bias,
           grads_ref, mix, dn_ref, un, inv,
           xs, gs, tilt, nm, q_s, k_s, v_s, dm_s, dq_s, dk_s, dv_s, fold):
    half_lat = WIN_LAT // 2
    half_lon = WIN_LON // 2

    pattern = base_pattern()
    fold[...] = jnp.zeros_like(fold)

    xs[...] = jnp.zeros_like(xs)
    gs[...] = jnp.zeros_like(gs)
    for w in range(windows):
        for r in range(WIN_LAT):
            at = w * TOK + r * PITCH
            start = half_lon + w * WIN_LON
            inside = WIN_LON if w < windows - 1 else half_lon
            for dst, lo in ((xs, 0), (gs, D)):
                if r < half_lat:
                    dst[at:at + inside, :] = own_ref[r + half_lat, start:start + inside, lo:lo + D]
                    if inside < WIN_LON:
                        dst[at + inside:at + WIN_LON, :] = side_ref[r, :, lo:lo + D]
                else:
                    dst[at:at + inside, :] = up_ref[r - half_lat, start:start + inside, lo:lo + D]
                    if inside < WIN_LON:
                        dst[at + inside:at + WIN_LON, :] = corner_ref[r - half_lat, :, lo:lo + D]

    gain = gain_ref[...]
    x = xs[...].astype(f32)
    centre = x - jnp.mean(x, axis=-1, keepdims=True)
    inverse = lax.rsqrt(jnp.mean(centre * centre, axis=-1, keepdims=True) + norm_eps)
    unit = centre * inverse
    un[...] = unit
    inv[...] = inverse
    normed = (unit * gain).astype(bf16)
    nm[...] = normed
    wq, wk, wv = (wqkv_ref[:, i * D:(i + 1) * D] for i in range(3))
    q_s[...] = nn(normed, wq).astype(bf16)
    k_s[...] = nn(normed, wk).astype(bf16)
    v_s[...] = nn(normed, wv).astype(bf16)
    dm_s[...] = nt(gs[...], wproj_ref[...]).astype(bf16)

    scale = HEAD ** (-0.5)
    head_of = iota((TOK, D), 1) // HEAD
    pads = jnp.zeros((LANES - TOK, D), bf16)

    def by_head(a):
        zero = jnp.zeros_like(a)
        return [jnp.where(head_of == h, a, zero) for h in range(HEADS)]

    def window(w):
        rows = pl.ds(w * TOK, TOK)
        kind = meta_ref[w]
        q, k, v, dm = q_s[rows, :], k_s[rows, :], v_s[rows, :], dm_s[rows, :]
        q_heads = jnp.concatenate(by_head(q), axis=0)
        dm_heads = jnp.concatenate(by_head(dm), axis=0)
        k_pad = jnp.concatenate([k, pads], axis=0)
        v_pad = jnp.concatenate([v, pads], axis=0)
        scores = nt(q_heads, k_pad) * scale + bias[kind]
        top = jnp.max(scores, axis=-1, keepdims=True)
        raised = jnp.exp(scores - top)
        probs = raised * (1.0 / jnp.sum(raised, axis=-1, keepdims=True))
        probs_low = probs.astype(bf16)
        d_probs = nt(dm_heads, v_pad)
        d_scores = probs * (d_probs - jnp.sum(probs * d_probs, axis=-1, keepdims=True))
        low = d_scores.astype(bf16)
        side = lambda a: jnp.concatenate([a[h * TOK:(h + 1) * TOK] for h in range(HEADS)], axis=1)
        tall = lambda a: jnp.concatenate([b for part in by_head(a) for b in (part, pads)], axis=0)
        mix[rows, :] = nn(side(probs_low), tall(v)).astype(bf16)
        dq_s[rows, :] = (nn(side(low), tall(k)) * scale).astype(bf16)
        dv_s[rows, :] = tn(probs_low, dm_heads)[:TOK].astype(bf16)
        dk_s[rows, :] = (tn(low, q_heads) * scale)[:TOK].astype(bf16)
        for h in range(HEADS):
            total = None
            for r in range(WIN_LAT):
                off = (WIN_LAT - 1 - r) * PITCH
                part = d_scores[h * TOK + r * PITCH:h * TOK + (r + 1) * PITCH]
                part = jnp.concatenate([part, jnp.zeros_like(part)], axis=1)
                if off:
                    part = pltpu.roll(part, off, axis=1)
                total = part if total is None else total + part
            fold[pl.ds(pl.multiple_of((h * kinds + kind) * PITCH, PITCH), PITCH), :] += total

    for w in range(windows):
        window(w)

    gp = tn(mix[...], gs[...]).astype(bf16)
    d_normed = nt(dq_s[...], wq) + nt(dk_s[...], wk) + nt(dv_s[...], wv)
    dn_ref[...] = d_normed
    gq = []
    for d in (dq_s, dk_s, dv_s):
        gq.append(tn(nm[...], d[...]).astype(bf16))
    gq = jnp.concatenate(gq, axis=1)
    for b in range(4):
        grads_ref[b * D:(b + 1) * D, :] = gq[:, b * LANES:(b + 1) * LANES]
    grads_ref[4 * D:5 * D, :] = jnp.concatenate([gq[:, 4 * LANES:], gp[:, LANES:]], axis=1)
    grads_ref[5 * D:6 * D, :] = gp[:, :LANES]
    unit = un[...]
    gg = jnp.sum(d_normed * unit, axis=0, keepdims=True)
    gg = jnp.concatenate([gg[:, :LANES], jnp.concatenate([gg[:, LANES:], jnp.zeros((1, SPAN - D), f32)], axis=1), jnp.zeros((ROWS - AT_GAIN - 2, LANES), f32)], axis=0)
    grads_ref[AT_GAIN:, :] = gg.astype(bf16)

    back = nt(fold[...], pattern, precision=highest)
    for half in range(2):
        tilt[half] = back[:, half * LANES:(half + 1) * LANES]
    total = None
    for c in range(WIN_LON):
        part = jnp.concatenate([tilt[half, pl.ds(c, kinds * HEADS, stride=PITCH), :] for half in range(2)], axis=1)
        if c:
            part = pltpu.roll(part, c, axis=1)
        total = part if total is None else total + part
    for half in range(2):
        at = AT_TABLE + half * kinds * HEADS
        grads_ref[at:at + kinds * HEADS, :] = total[:, half * LANES:(half + 1) * LANES].astype(bf16)


def results_kernel(windows, mix, dn_ref, un, inv, gain_ref, wproj_ref, both_ref):
    gain = gain_ref[...]
    branch = nn(mix[...], wproj_ref[...]).astype(bf16)
    d_normed = dn_ref[...]
    unit = un[...]
    d_unit = d_normed * gain
    path = inv[...] * (d_unit - jnp.mean(d_unit, axis=-1, keepdims=True) - unit * jnp.mean(d_unit * unit, axis=-1, keepdims=True))
    path = path.astype(bf16)
    for w in range(windows):
        for r in range(WIN_LAT):
            at = w * TOK + r * PITCH
            both_ref[r, w * WIN_LON:(w + 1) * WIN_LON, 0:D] = branch[at:at + WIN_LON]
            both_ref[r, w * WIN_LON:(w + 1) * WIN_LON, D:2 * D] = path[at:at + WIN_LON]


def results(windows, mix, d_normed, unit, inverse, gain, w_proj):
    vm = pl.BlockSpec(memory_space=pltpu.VMEM)
    return pl.pallas_call(
        functools.partial(results_kernel, windows),
        out_shape=jax.ShapeDtypeStruct((WIN_LAT, windows * WIN_LON, 2 * D), bf16),
        in_specs=[vm] * 6,
        out_specs=vm,
        cost_estimate=pl.CostEstimate(flops=60_000_000, bytes_accessed=2_000_000, transcendentals=0),
        compiler_params=pltpu.CompilerParams(vmem_limit_bytes=VM_RESULTS << 20),
        name="results",
    )(mix, d_normed, unit, inverse, gain, w_proj)


def attend(kinds, own, up, side, corner, gain, w_qkv, w_proj, bias):
    windows = own.shape[1] // WIN_LON
    n = windows * TOK
    vm = pl.BlockSpec(memory_space=pltpu.VMEM)
    kh = bias.shape[0] * HEADS
    return pl.pallas_call(
        functools.partial(kernel, windows, bias.shape[0]),
        out_shape=(
            jax.ShapeDtypeStruct((ROWS, LANES), bf16),
            jax.ShapeDtypeStruct((n, D), bf16),
            jax.ShapeDtypeStruct((n, D), f32),
            jax.ShapeDtypeStruct((n, D), f32),
            jax.ShapeDtypeStruct((n, 1), f32),
        ),
        in_specs=[pl.BlockSpec(memory_space=pltpu.SMEM)] + [vm] * 8,
        out_specs=(vm,) * 5,
        scratch_shapes=[
            pltpu.VMEM((n, D), bf16), pltpu.VMEM((n, D), bf16), pltpu.VMEM((2, kh * PITCH, LANES), f32),
            pltpu.VMEM((n, D), bf16),
        ] + [pltpu.VMEM((n, D), bf16)] * 7 + [pltpu.VMEM((kh * PITCH, SPAN), f32)],
        cost_estimate=pl.CostEstimate(flops=2_000_000_000, bytes_accessed=4_000_000, transcendentals=500_000),
        compiler_params=pltpu.CompilerParams(vmem_limit_bytes=VM_ATTEND << 20),
        name="attend",
    )(kinds, own, up, side, corner, gain, w_qkv, w_proj, bias)


def finish_kernel(grads_ref, gq_ref, gp_ref, gt_ref, gg_ref):
    def scale_of(parts, count):
        total = sum(jnp.sum(jnp.sum(p * p, axis=0, keepdims=True), axis=1, keepdims=True) for p in parts)
        return jnp.minimum(1.0, lax.rsqrt(total / count + clip_eps))

    kh = gt_ref.shape[0]
    wide = [grads_ref[b * D:(b + 1) * D, :].astype(f32) for b in range(4)]
    shared = grads_ref[4 * D:5 * D, :].astype(f32)
    low, high = shared[:, :LANES // 2], shared[:, LANES // 2:]
    first = grads_ref[5 * D:6 * D, :].astype(f32)
    by = scale_of(wide + [low], gq_ref.shape[0] * gq_ref.shape[1])
    for b in range(4):
        gq_ref[:, b * LANES:(b + 1) * LANES] = wide[b] * by
    gq_ref[:, 4 * LANES:] = low * by
    by = scale_of([first, high], gp_ref.shape[0] * gp_ref.shape[1])
    gp_ref[:, :LANES] = first * by
    gp_ref[:, LANES:] = high * by
    left = grads_ref[AT_TABLE:AT_TABLE + kh, :].astype(f32)
    right = grads_ref[AT_TABLE + kh:AT_TABLE + 2 * kh, :].astype(f32)
    by = scale_of([left, right], kh * gt_ref.shape[1])
    gt_ref[:, :LANES] = left * by
    gt_ref[:, LANES:] = (right * by)[:, :gt_ref.shape[1] - LANES]
    rows = grads_ref[AT_GAIN:AT_GAIN + 16, :].astype(f32)
    by = scale_of([rows], D)
    gg_ref[:, :LANES] = rows[0:1] * by
    gg_ref[:, LANES:] = (rows[1:2] * by)[:, :D - LANES]


def finish(grads, table_rows, extent):
    vm = pl.BlockSpec(memory_space=pltpu.VMEM)
    return pl.pallas_call(
        finish_kernel,
        out_shape=(
            jax.ShapeDtypeStruct((D, 3 * D), f32),
            jax.ShapeDtypeStruct((D, D), f32),
            jax.ShapeDtypeStruct((table_rows, extent), f32),
            jax.ShapeDtypeStruct((1, D), f32),
        ),
        in_specs=[vm],
        out_specs=(vm,) * 4,
        cost_estimate=pl.CostEstimate(flops=1_000_000, bytes_accessed=1_000_000, transcendentals=4),
        compiler_params=pltpu.CompilerParams(vmem_limit_bytes=VM_FINISH << 20),
        name="finish",
    )(grads)


def shifted(value, axis, steps):
    count = lax.axis_size(axis)
    return lax.ppermute(value, axis, [(i, (i + steps) % count) for i in range(count)])


def exchange(part, axes):
    return lax.all_to_all(part, axes, 0, 0, tiled=True)


def whole_sum(got):
    return jnp.sum(got.astype(f32), axis=0).astype(bf16)


def copies(part, axes):
    return jnp.broadcast_to(part[None], (lax.axis_size(axes),) + part.shape)


def total_of(packed):
    part = exchange(packed.reshape(lax.axis_size(SLICED), -1, LANES), SLICED)
    part = whole_sum(part)
    part = exchange(copies(part, WHOLE), WHOLE)
    part = whole_sum(part)
    part = exchange(copies(part, SLICED), SLICED)
    return part.reshape(-1, LANES)


def on_device(state_grid, norm_gain, w_qkv, w_proj, bias_table, window_kind, cotangent):
    _, cols_dev, channels = state_grid.shape
    half_lat, half_lon = WIN_LAT // 2, WIN_LON // 2
    lat, lon = lax.axis_index(LAT), lax.axis_index(LON)
    windows = cols_dev // WIN_LON
    joint = lax.optimization_barrier(jnp.concatenate([state_grid, cotangent], axis=2))
    side = joint[half_lat:, :half_lon]
    up = shifted(joint[:half_lat], LAT, -1)
    lats, lons = lax.axis_size(LAT), lax.axis_size(LON)
    before = [(i * lons + j, (i - 1) % lats * lons + (j - 1) % lons) for i in range(lats) for j in range(lons)]
    corner = lax.ppermute(joint[:half_lat, :half_lon], LAT + LON, before)
    side = shifted(side, LON, -1)
    kinds = lax.dynamic_slice(window_kind, (lat, lon * windows), (1, windows))[0]
    last = (lat == lax.axis_size(LAT) - 1).astype(jnp.int32)
    kind_count, heads, extent = bias_table.shape
    table = bias_table.transpose(1, 0, 2).reshape(heads * kind_count, extent)
    gain = norm_gain.reshape(1, -1)
    packed, *kept = attend(kinds, joint, up, side, corner, gain, w_qkv, w_proj, bias_of(table, last[None]))
    both = results(windows, *kept, gain, w_proj)
    moved = shifted(both[:, -half_lon:], LON, 1)
    placed = jnp.concatenate([moved, both[:, :-half_lon]], axis=1)
    lower = shifted(placed[half_lat:], LAT, 1)
    summed = total_of(packed)
    own = jnp.concatenate([lower, placed[:half_lat]], axis=0).astype(f32)
    out_field = (state_grid.astype(f32) + own[:, :, :channels]).astype(bf16)
    d_field = (cotangent.astype(f32) + own[:, :, channels:]).astype(bf16)
    gq, gp, gt, gg = finish(summed, heads * kind_count, extent)
    gt = gt.reshape(heads, kind_count, extent).transpose(1, 0, 2)
    return (out_field, d_field, gq, gp, gt, gg.reshape(-1))


def solution(mesh):
    in_specs = (P(LAT, LON, None), P(), P(), P(), P(), P(), P(LAT, LON, None))
    out_specs = (P(LAT, LON, None), P(LAT, LON, None), P(), P(), P(), P())
    mesh = Mesh(mesh.devices.reshape(PARTS), LAT + LON)
    return jax.shard_map(on_device, mesh=mesh, in_specs=in_specs, out_specs=out_specs, check_vma=False)
```

profile of v0, /device:TPU:1, one launch (start us, length us, event | category | flops | bytes accessed | tf_op | source)
XLA Modules:
  0.0 86.4 jit_solution(5111605390040541901)
XLA Ops:
  0.6 0.0 copy-start
  0.6 0.0 copy-start.1
  0.7 1.2 %pad_maximum_fusion.1.own_ref = bf16[6,84,384]{2,1,0:T(8,128)(2,1)S(1)} fusion(bf16[6,84,192]{2,1,0:T(8,128)(2,1)} %param.13, bf16[6,84,192]{2,1,0:T(8,128)(2,1)} %param.7), kind=kLoop, calls=%fused_computation.7 | loop fusion | flops 774144 | bytes 774144 | tf_op jit(solution)/shard_map/concatenate | solution.py:357
  2.0 12.5 %collective-permute-start = (bf16[3,84,384]{2,1,0:T(8,128)(2,1)S(1)}, bf16[3,84,384]{2,1,0:T(8,128)(2,1)S(1)}, u32[]{:S(2)}, u32[]{:S(2)}) collective-permute-start(bf16[3,84,384]{2,1,0:T(8,128)(2,1)S(1)} %slice.36), channel_id=1, source_target_pairs={{0,480},{32,0},{64,32},{96,64},{128,96},{160,128},{192,160},{224,1... | collective-permute-start | bytes 580616 | tf_op jit(solution)/shard_map/ppermute | solution.py:328
  14.5 3.0 %collective-permute-start.2 = (bf16[3,6,384]{2,1,0:T(8,128)(2,1)S(1)}, bf16[3,6,384]{2,1,0:T(8,128)(2,1)S(1)}, u32[]{:S(2)}, u32[]{:S(2)}) collective-permute-start(bf16[3,6,384]{2,1,0:T(8,128)(2,1)S(1)} %get-tuple-element.26), channel_id=1, source_target_pairs={{0,511},{1,480},{2,481},{3,482},{4,483},{5,484},{6,485},{7,486},{8... | collective-permute-start | bytes 41480 | tf_op jit(solution)/shard_map/ppermute | solution.py:362
  17.5 5.5 %collective-permute-start.1 = (bf16[3,6,384]{2,1,0:T(8,128)(2,1)S(1)}, bf16[3,6,384]{2,1,0:T(8,128)(2,1)S(1)}, u32[]{:S(2)}, u32[]{:S(2)}) collective-permute-start(bf16[3,6,384]{2,1,0:T(8,128)(2,1)S(1)} %get-tuple-element.27), channel_id=1, source_target_pairs={{0,31},{1,0},{2,1},{3,2},{4,3},{5,4},{6,5},{7,6},{8,7},{9,8},{10,9... | collective-permute-start | bytes 41480 | tf_op jit(solution)/shard_map/ppermute | solution.py:328
  23.1 0.1 dynamic-slice_bitcast_fusion.meta_ref
  23.2 0.8 copy-done.2
  24.0 2.1 %bias.1 = f32[8,576,128]{2,1,0:T(8,128)S(1)} custom-call(f32[48,253]{1,0:T(8,128)S(1)} %bitcast.15, s32[1]{0:T(128)} %bitcast.4.last_ref), custom_call_target="tpu_custom_call" | custom-call | flops 600000000 | bytes 2500000 | tf_op jit(solution)/shard_map/bias/pallas_call | solution.py:97
  26.1 0.0 collective-permute-done.2.corner_ref
  26.1 0.0 collective-permute-done.1.side_ref
  26.1 0.0 collective-permute-done.up_ref
  26.2 7.6 %attend.1 = (bf16[1280,128]{1,0:T(8,128)(2,1)S(1)}, bf16[672,192]{1,0:T(8,128)(2,1)S(1)}, f32[672,192]{1,0:T(8,128)S(1)}, f32[672,192]{1,0:T(8,128)S(1)}, f32[672,1]{1,0:T(8,128)S(1)}) custom-call(s32[7]{0:T(128)S(1)} %dynamic-slice_bitcast_fusion.meta_ref, bf16[6,84,384]{2,1,0:T(8,128)(2,1)S(1)} %pad_maximum_fusion.1.own_ref, ...), custom_call_target="tpu_custom_call" | custom-call | flops 2000000000 | bytes 4000000 | tf_op jit(solution)/shard_map/attend/pallas_call | solution.py:259
  33.8 14.5 %all_to_all.15 = bf16[32,40,128]{2,1,0:T(8,128)(2,1)S(1)} all-to-all(bf16[32,40,128]{2,1,0:T(8,128)(2,1)S(1)} %bitcast.14), channel_id=1, replica_groups=mesh['y_lo'=2,'z_hi'=4,'z_lo'=2,'y_hi'=4,'x'=4,'core'=2] {'y_lo','z_lo',..., dimensions={0} | all-to-all | bytes 655360 | tf_op jit(solution)/shard_map/all_to_all | solution.py:332
  48.3 0.1 reduce_sum.24
  48.4 0.7 broadcast_in_dim.19
  49.1 5.8 %all-to-all-start.1 = ((bf16[16,40,128]{2,1,0:T(8,128)(2,1)}), bf16[16,40,128]{2,1,0:T(8,128)(2,1)S(1)}, u32[]{:S(2)}, u32[]{:S(2)}) async-start(bf16[16,40,128]{2,1,0:T(8,128)(2,1)} %broadcast_in_dim.19), calls=%async_computation.1 | async-start | bytes 327680 | tf_op jit(solution)/shard_map/all_to_all | solution.py:332
  54.8 0.6 results.1
  55.4 0.0 copy-start.5
  55.4 0.0 copy-start.6
  55.4 2.7 %collective-permute-start.3 = (bf16[6,6,384]{2,1,0:T(8,128)(2,1)S(1)}, bf16[6,6,384]{2,1,0:T(8,128)(2,1)S(1)}, u32[]{:S(2)}, u32[]{:S(2)}) collective-permute-start(bf16[6,6,384]{2,1,0:T(8,128)(2,1)S(1)} %slice.39), channel_id=1, source_target_pairs={{0,1},{1,2},{2,3},{3,4},{4,5},{5,6},{6,7},{7,8},{8,9},{9,10},{10,1... | collective-permute-start | bytes 82952 | tf_op jit(solution)/shard_map/ppermute | solution.py:328
  58.2 8.0 %all-to-all-done.1 = bf16[16,40,128]{2,1,0:T(8,128)(2,1)S(1)} async-done(((bf16[16,40,128]{2,1,0:T(8,128)(2,1)}), bf16[16,40,128]{2,1,0:T(8,128)(2,1)S(1)}, u32[]{:S(2)}, u32[]{:S(2)}) %all-to-all-start.1) | async-done | bytes 163872 | tf_op jit(solution)/shard_map/all_to_all | solution.py:332
  66.3 0.8 broadcast_in_dim.20
  67.0 5.3 %all-to-all-start.2 = ((bf16[32,40,128]{2,1,0:T(8,128)(2,1)}), bf16[32,40,128]{2,1,0:T(8,128)(2,1)S(1)}, u32[]{:S(2)}, u32[]{:S(2)}) async-start(bf16[32,40,128]{2,1,0:T(8,128)(2,1)} %broadcast_in_dim.20), calls=%async_computation.2 | async-start | bytes 655360 | tf_op jit(solution)/shard_map/all_to_all | solution.py:332
  72.3 0.0 collective-permute-done.3
  72.3 0.1 fusion.4
  72.4 3.3 %collective-permute-start.4 = (bf16[3,84,384]{2,1,0:T(8,128)(2,1)S(1)}, bf16[3,84,384]{2,1,0:T(8,128)(2,1)S(1)}, u32[]{:S(2)}, u32[]{:S(2)}) collective-permute-start(bf16[3,84,384]{2,1,0:T(8,128)(2,1)S(1)} %fusion.4), channel_id=1, source_target_pairs={{0,32},{32,64},{64,96},{96,128},{128,160},{160,192},{192,224},{224... | collective-permute-start | bytes 580616 | tf_op jit(solution)/shard_map/ppermute | solution.py:328
  75.7 8.5 %collective-permute-done.4 = bf16[3,84,384]{2,1,0:T(8,128)(2,1)S(1)} collective-permute-done((bf16[3,84,384]{2,1,0:T(8,128)(2,1)S(1)}, bf16[3,84,384]{2,1,0:T(8,128)(2,1)S(1)}, u32[]{:S(2)}, u32[]{:S(2)}) %collective-permute-start.4) | collective-permute-done | bytes 193568 | tf_op jit(solution)/shard_map/ppermute | solution.py:328
  84.2 0.1 fusion.3
  84.3 1.0 %fusion = (bf16[6,84,192]{2,1,0:T(8,128)(2,1)}, bf16[6,84,192]{2,1,0:T(8,128)(2,1)}) fusion(f32[6,84,384]{2,1,0:T(8,128)S(1)} %fusion.3, bf16[6,84,192]{2,1,0:T(8,128)(2,1)S(1)} %copy-done.5, bf16[6,84,192]{2,1,0:T(8,128)(2,1)S(1)} %copy-done.6), kind=kLoop, calls=%fused_computation.1 | loop fusion | flops 580608 | bytes 1548288 | tf_op jit(solution)/shard_map/convert_element_type | solution.py:377
  85.3 0.0 all-to-all-done.2
  85.3 1.1 %finish.1 = (f32[192,576]{1,0:T(8,128)}, f32[192,192]{1,0:T(8,128)}, f32[48,253]{1,0:T(8,128)}, f32[1,192]{1,0:T(1,128)}) custom-call(bf16[1280,128]{1,0:T(8,128)(2,1)S(1)} %bitcast.13), custom_call_target="tpu_custom_call" | custom-call | flops 1000000 | bytes 1000000 | tf_op jit(solution)/shard_map/finish/pallas_call | solution.py:310
  (14 shorter events, 0.1 us)
Async XLA Ops:
  0.6 22.4 %copy-start = (s32[16,224]{1,0:T(8,128)S(1)}, s32[16,224]{1,0:T(8,128)}, u32[]{:S(2)}) copy-start(s32[16,224]{1,0:T(8,128)} %param.12) | copy-start | bytes 43012
  0.6 25.5 %copy-start.1 = (bf16[192,192]{1,0:T(8,128)(2,1)S(1)}, bf16[192,192]{1,0:T(8,128)(2,1)}, u32[]{:S(2)}) copy-start(bf16[192,192]{1,0:T(8,128)(2,1)} %wproj_ref.3) | copy-start | bytes 221188
  0.7 25.5 %copy-start.4 = (bf16[192,576]{1,0:T(8,128)(2,1)S(1)}, bf16[192,576]{1,0:T(8,128)(2,1)}, u32[]{:S(2)}) copy-start(bf16[192,576]{1,0:T(8,128)(2,1)} %wqkv_ref.1) | copy-start | bytes 663556
  0.7 25.5 %copy-start.3 = (f32[192]{0:T(256)S(1)}, f32[192]{0:T(256)}, u32[]{:S(2)}) copy-start(f32[192]{0:T(256)} %param.8) | copy-start | bytes 2308
  2.0 24.2 %collective-permute-start = (bf16[3,84,384]{2,1,0:T(8,128)(2,1)S(1)}, bf16[3,84,384]{2,1,0:T(8,128)(2,1)S(1)}, u32[]{:S(2)}, u32[]{:S(2)}) collective-permute-start(bf16[3,84,384]{2,1,0:T(8,128)(2,1)S(1)} %slice.36), channel_id=1, source_target_pairs={{0,480},{32,0},{64,32},{96,64},{128,96},{160,128},{192,160},{224,1... | collective-permute-start | bytes 580616 | tf_op jit(solution)/shard_map/ppermute | solution.py:328
  14.5 11.6 %collective-permute-start.2 = (bf16[3,6,384]{2,1,0:T(8,128)(2,1)S(1)}, bf16[3,6,384]{2,1,0:T(8,128)(2,1)S(1)}, u32[]{:S(2)}, u32[]{:S(2)}) collective-permute-start(bf16[3,6,384]{2,1,0:T(8,128)(2,1)S(1)} %get-tuple-element.26), channel_id=1, source_target_pairs={{0,511},{1,480},{2,481},{3,482},{4,483},{5,484},{6,485},{7,486},{8... | collective-permute-start | bytes 41480 | tf_op jit(solution)/shard_map/ppermute | solution.py:362
  17.5 8.6 %collective-permute-start.1 = (bf16[3,6,384]{2,1,0:T(8,128)(2,1)S(1)}, bf16[3,6,384]{2,1,0:T(8,128)(2,1)S(1)}, u32[]{:S(2)}, u32[]{:S(2)}) collective-permute-start(bf16[3,6,384]{2,1,0:T(8,128)(2,1)S(1)} %get-tuple-element.27), channel_id=1, source_target_pairs={{0,31},{1,0},{2,1},{3,2},{4,3},{5,4},{6,5},{7,6},{8,7},{9,8},{10,9... | collective-permute-start | bytes 41480 | tf_op jit(solution)/shard_map/ppermute | solution.py:328
  23.2 0.8 copy-start.2
  49.1 17.2 %all-to-all-start.1 = ((bf16[16,40,128]{2,1,0:T(8,128)(2,1)}), bf16[16,40,128]{2,1,0:T(8,128)(2,1)S(1)}, u32[]{:S(2)}, u32[]{:S(2)}) async-start(bf16[16,40,128]{2,1,0:T(8,128)(2,1)} %broadcast_in_dim.19), calls=%async_computation.1 | async-start | bytes 327680 | tf_op jit(solution)/shard_map/all_to_all | solution.py:332
  55.4 28.9 %copy-start.5 = (bf16[6,84,192]{2,1,0:T(8,128)(2,1)S(1)}, bf16[6,84,192]{2,1,0:T(8,128)(2,1)}, u32[]{:S(2)}) copy-start(bf16[6,84,192]{2,1,0:T(8,128)(2,1)} %param.13) | copy-start | bytes 580612
  55.4 28.9 %copy-start.6 = (bf16[6,84,192]{2,1,0:T(8,128)(2,1)S(1)}, bf16[6,84,192]{2,1,0:T(8,128)(2,1)}, u32[]{:S(2)}) copy-start(bf16[6,84,192]{2,1,0:T(8,128)(2,1)} %param.7) | copy-start | bytes 580612
  55.4 16.9 %collective-permute-start.3 = (bf16[6,6,384]{2,1,0:T(8,128)(2,1)S(1)}, bf16[6,6,384]{2,1,0:T(8,128)(2,1)S(1)}, u32[]{:S(2)}, u32[]{:S(2)}) collective-permute-start(bf16[6,6,384]{2,1,0:T(8,128)(2,1)S(1)} %slice.39), channel_id=1, source_target_pairs={{0,1},{1,2},{2,3},{3,4},{4,5},{5,6},{6,7},{7,8},{8,9},{9,10},{10,1... | collective-permute-start | bytes 82952 | tf_op jit(solution)/shard_map/ppermute | solution.py:328
  67.0 18.3 %all-to-all-start.2 = ((bf16[32,40,128]{2,1,0:T(8,128)(2,1)}), bf16[32,40,128]{2,1,0:T(8,128)(2,1)S(1)}, u32[]{:S(2)}, u32[]{:S(2)}) async-start(bf16[32,40,128]{2,1,0:T(8,128)(2,1)} %broadcast_in_dim.20), calls=%async_computation.2 | async-start | bytes 655360 | tf_op jit(solution)/shard_map/all_to_all | solution.py:332
  72.4 11.8 %collective-permute-start.4 = (bf16[3,84,384]{2,1,0:T(8,128)(2,1)S(1)}, bf16[3,84,384]{2,1,0:T(8,128)(2,1)S(1)}, u32[]{:S(2)}, u32[]{:S(2)}) collective-permute-start(bf16[3,84,384]{2,1,0:T(8,128)(2,1)S(1)} %fusion.4), channel_id=1, source_target_pairs={{0,32},{32,64},{64,96},{96,128},{128,160},{160,192},{192,224},{224... | collective-permute-start | bytes 580616 | tf_op jit(solution)/shard_map/ppermute | solution.py:328
where the time goes:
time: 86.9 us; the launch traced here: 86.4 us
  starting transfers between devices  38.1 us (44%)
  waiting for transfers between devices  16.5 us (19%)
  blocking collectives  14.5 us (17%)
  Pallas kernels  11.4 us (13%)
  other arithmetic  2.51 us (3%)
  local copies, waits for them, and re-layouts  2.45 us (3%)
  between operations  0.91 us (1%)
    ppermute x4, starting transfers between devices, shifted(): lax.ppermute(value, axis, [(i, (i + steps) % count) for i in range(count)])  24.1 us
    all_to_all x1, blocking collectives, exchange(): return lax.all_to_all(part, axes, 0, 0, tiled=True)  14.5 us
    all_to_all x2, starting transfers between devices, exchange(): return lax.all_to_all(part, axes, 0, 0, tiled=True)  11 us
    ppermute x4, waiting for transfers between devices, shifted(): lax.ppermute(value, axis, [(i, (i + steps) % count) for i in range(count)])  8.47 us
    all_to_all x2, waiting for transfers between devices, exchange(): return lax.all_to_all(part, axes, 0, 0, tiled=True)  8.02 us
    pallas_call x1, Pallas kernels, attend(): pl.pallas_call(functools.partial(kernel, windows, bias.shape[0]), out_sha...  7.65 us
    ppermute x1, starting transfers between devices, on_device(): corner = lax.ppermute(joint[:half_lat, :half_lon], LAT + LON, before)  3.02 us
    pallas_call x1, Pallas kernels, bias_of(): pl.pallas_call(bias_kernel, out_shape=jax.ShapeDtypeStruct((kh // HEADS,...  2.13 us
  transfers between devices with their start and end apart: 7, of which 2 were waited for; matrix products, arithmetic and copies ran while one was open for 2% of the time, Pallas kernels for 3%

commit v1 on v0

--- a/solution.py
+++ b/solution.py
@@ -30,7 +30,6 @@
 PARTS = (2, 4, 2, 4, 4, 2)
 SLICED = ("y_lo", "z_lo", "x", "core")
 WHOLE = ("z_hi", "y_hi")
-highest = lax.Precision.HIGHEST
 f32 = jnp.float32
 bf16 = jnp.bfloat16
 
@@ -73,7 +72,13 @@
         for half in range(2):
             tilt[half, pl.ds(c, kinds * HEADS, stride=PITCH), :] = moved[:, half * LANES:(half + 1) * LANES]
     pattern = base_pattern()
-    span[...] = nn(jnp.concatenate([tilt[0], tilt[1]], axis=1), pattern, precision=highest)
+    whole = jnp.concatenate([tilt[0], tilt[1]], axis=1)
+    parts = []
+    for _ in range(3):
+        parts.append(whole.astype(bf16))
+        whole = whole - parts[-1].astype(f32)
+    pattern = pattern.astype(bf16)
+    span[...] = nn(jnp.concatenate(parts, axis=1), jnp.concatenate([pattern] * 3, axis=0))
     slot = iota((PITCH, LANES), 1)
     open_slot = (slot % PITCH < WIN_LON) & (slot < TOK)
     split = last_ref[0] > 0
@@ -82,10 +87,14 @@
         wide = span[pl.ds(pl.multiple_of(n * PITCH, PITCH), PITCH), :]
         for r in range(WIN_LAT):
             off = (WIN_LAT - 1 - r) * PITCH
-            part = wide if off == 0 else pltpu.roll(wide, SPAN - off, axis=1)
+            part = wide[:, :LANES]
+            if off:
+                part = pltpu.roll(part, LANES - off, axis=1)
+            if off + TOK > LANES:
+                part = jnp.where(slot < LANES - off, part, pltpu.roll(wide[:, LANES:], LANES - off, axis=1))
             other = (slot < half_lat * PITCH) if r >= half_lat else (slot >= half_lat * PITCH)
             ok = open_slot & jnp.logical_not(split & other)
-            bias[n % kinds, pl.ds(pl.multiple_of((n // kinds) * TOK + r * PITCH, PITCH), PITCH), :] = jnp.where(ok, part[:, :LANES], masked)
+            bias[n % kinds, pl.ds(pl.multiple_of((n // kinds) * TOK + r * PITCH, PITCH), PITCH), :] = jnp.where(ok, part, masked)
         return carry
 
     lax.fori_loop(0, kinds * HEADS, spread, 0, unroll=True)
@@ -149,6 +158,7 @@
     v_s[...] = nn(normed, wv).astype(bf16)
     dm_s[...] = nt(gs[...], wproj_ref[...]).astype(bf16)
 
+    key_slot = iota((PITCH, LANES), 1)
     scale = HEAD ** (-0.5)
     head_of = iota((TOK, D), 1) // HEAD
     pads = jnp.zeros((LANES - TOK, D), bf16)
@@ -180,15 +190,20 @@
         dv_s[rows, :] = tn(probs_low, dm_heads)[:TOK].astype(bf16)
         dk_s[rows, :] = (tn(low, q_heads) * scale)[:TOK].astype(bf16)
         for h in range(HEADS):
-            total = None
+            left = right = jnp.zeros((PITCH, LANES), f32)
             for r in range(WIN_LAT):
                 off = (WIN_LAT - 1 - r) * PITCH
                 part = d_scores[h * TOK + r * PITCH:h * TOK + (r + 1) * PITCH]
-                part = jnp.concatenate([part, jnp.zeros_like(part)], axis=1)
                 if off:
                     part = pltpu.roll(part, off, axis=1)
-                total = part if total is None else total + part
-            fold[pl.ds(pl.multiple_of((h * kinds + kind) * PITCH, PITCH), PITCH), :] += total
+                if off + TOK > LANES:
+                    over = key_slot < off + TOK - LANES
+                    right = right + jnp.where(over, part, 0.0)
+                    part = jnp.where(over, 0.0, part)
+                left = left + part
+            at = pl.ds(pl.multiple_of((h * kinds + kind) * PITCH, PITCH), PITCH)
+            fold[at, :LANES] += left
+            fold[at, LANES:] += right
 
     for w in range(windows):
         window(w)
@@ -209,9 +224,14 @@
     gg = jnp.concatenate([gg[:, :LANES], jnp.concatenate([gg[:, LANES:], jnp.zeros((1, SPAN - D), f32)], axis=1), jnp.zeros((ROWS - AT_GAIN - 2, LANES), f32)], axis=0)
     grads_ref[AT_GAIN:, :] = gg.astype(bf16)
 
-    back = nt(fold[...], pattern, precision=highest)
-    for half in range(2):
-        tilt[half] = back[:, half * LANES:(half + 1) * LANES]
+    low_pattern = pattern.astype(bf16)
+    step = kinds * PITCH
+    for h in range(HEADS):
+        part = fold[h * step:(h + 1) * step, :]
+        high = part.astype(bf16)
+        back = nt(jnp.concatenate([high, (part - high.astype(f32)).astype(bf16)], axis=1), jnp.concatenate([low_pattern, low_pattern], axis=1))
+        for half in range(2):
+            tilt[half, h * step:(h + 1) * step, :] = back[:, half * LANES:(half + 1) * LANES]
     total = None
     for c in range(WIN_LON):
         part = jnp.concatenate([tilt[half, pl.ds(c, kinds * HEADS, stride=PITCH), :] for half in range(2)], axis=1)

time: 86.9 us -> 86.7 us (level)
  transfers between devices with their start and end apart: 7 -> 7, of which waited for: 2 -> 2; matrix products, arithmetic and copies ran while one was open for 2% -> 2% of each run, Pallas kernels for 3% -> 2%
where the time goes in v1:
time: 86.7 us; the launch traced here: 86.2 us
  starting transfers between devices  38.7 us (45%)
  waiting for transfers between devices  16.5 us (19%)
  blocking collectives  14.5 us (17%)
  Pallas kernels  10.7 us (12%)
  other arithmetic  2.51 us (3%)
  local copies, waits for them, and re-layouts  2.45 us (3%)
  between operations  0.91 us (1%)
    ppermute x4, starting transfers between devices, shifted(): lax.ppermute(value, axis, [(i, (i + steps) % count) for i in range(count)])  24.1 us
    all_to_all x1, blocking collectives, exchange(): return lax.all_to_all(part, axes, 0, 0, tiled=True)  14.5 us
    all_to_all x2, starting transfers between devices, exchange(): return lax.all_to_all(part, axes, 0, 0, tiled=True)  11.6 us
    ppermute x4, waiting for transfers between devices, shifted(): lax.ppermute(value, axis, [(i, (i + steps) % count) for i in range(count)])  8.47 us
    all_to_all x2, waiting for transfers between devices, exchange(): return lax.all_to_all(part, axes, 0, 0, tiled=True)  8.02 us
    pallas_call x1, Pallas kernels, attend(): pl.pallas_call(functools.partial(kernel, windows, bias.shape[0]), out_sha...  7.47 us
    ppermute x1, starting transfers between devices, on_device(): corner = lax.ppermute(joint[:half_lat, :half_lon], LAT + LON, before)  3.02 us
  transfers between devices with their start and end apart: 7, of which 2 were waited for; matrix products, arithmetic and copies ran while one was open for 2% of the time, Pallas kernels for 2%

profile of v1, /device:TPU:1, one launch (start us, length us, event | category | flops | bytes accessed | tf_op | source)
XLA Modules:
  0.0 86.2 jit_solution(5082921676296146877)
XLA Ops:
  0.6 0.0 copy-start
  0.6 0.0 copy-start.1
  0.7 1.2 %pad_maximum_fusion.1.own_ref = bf16[6,84,384]{2,1,0:T(8,128)(2,1)S(1)} fusion(bf16[6,84,192]{2,1,0:T(8,128)(2,1)} %param.13, bf16[6,84,192]{2,1,0:T(8,128)(2,1)} %param.7), kind=kLoop, calls=%fused_computation.7 | loop fusion | flops 774144 | bytes 774144 | tf_op jit(solution)/shard_map/concatenate | solution.py:377
  2.0 12.5 %collective-permute-start = (bf16[3,84,384]{2,1,0:T(8,128)(2,1)S(1)}, bf16[3,84,384]{2,1,0:T(8,128)(2,1)S(1)}, u32[]{:S(2)}, u32[]{:S(2)}) collective-permute-start(bf16[3,84,384]{2,1,0:T(8,128)(2,1)S(1)} %slice.36), channel_id=1, source_target_pairs={{0,480},{32,0},{64,32},{96,64},{128,96},{160,128},{192,160},{224,1... | collective-permute-start | bytes 580616 | tf_op jit(solution)/shard_map/ppermute | solution.py:348
  14.5 3.0 %collective-permute-start.2 = (bf16[3,6,384]{2,1,0:T(8,128)(2,1)S(1)}, bf16[3,6,384]{2,1,0:T(8,128)(2,1)S(1)}, u32[]{:S(2)}, u32[]{:S(2)}) collective-permute-start(bf16[3,6,384]{2,1,0:T(8,128)(2,1)S(1)} %get-tuple-element.26), channel_id=1, source_target_pairs={{0,511},{1,480},{2,481},{3,482},{4,483},{5,484},{6,485},{7,486},{8... | collective-permute-start | bytes 41480 | tf_op jit(solution)/shard_map/ppermute | solution.py:382
  17.5 5.5 %collective-permute-start.1 = (bf16[3,6,384]{2,1,0:T(8,128)(2,1)S(1)}, bf16[3,6,384]{2,1,0:T(8,128)(2,1)S(1)}, u32[]{:S(2)}, u32[]{:S(2)}) collective-permute-start(bf16[3,6,384]{2,1,0:T(8,128)(2,1)S(1)} %get-tuple-element.27), channel_id=1, source_target_pairs={{0,31},{1,0},{2,1},{3,2},{4,3},{5,4},{6,5},{7,6},{8,7},{9,8},{10,9... | collective-permute-start | bytes 41480 | tf_op jit(solution)/shard_map/ppermute | solution.py:348
  23.1 0.1 dynamic-slice_bitcast_fusion.meta_ref
  23.2 0.8 copy-done.2
  24.0 1.6 %bias.1 = f32[8,576,128]{2,1,0:T(8,128)S(1)} custom-call(f32[48,253]{1,0:T(8,128)S(1)} %bitcast.15, s32[1]{0:T(128)} %bitcast.4.last_ref), custom_call_target="tpu_custom_call" | custom-call | flops 600000000 | bytes 2500000 | tf_op jit(solution)/shard_map/bias/pallas_call | solution.py:106
  25.6 0.0 collective-permute-done.2.corner_ref
  25.6 0.0 collective-permute-done.1.side_ref
  25.6 0.0 collective-permute-done.up_ref
  25.6 7.5 %attend.1 = (bf16[1280,128]{1,0:T(8,128)(2,1)S(1)}, bf16[672,192]{1,0:T(8,128)(2,1)S(1)}, f32[672,192]{1,0:T(8,128)S(1)}, f32[672,192]{1,0:T(8,128)S(1)}, f32[672,1]{1,0:T(8,128)S(1)}) custom-call(s32[7]{0:T(128)S(1)} %dynamic-slice_bitcast_fusion.meta_ref, bf16[6,84,384]{2,1,0:T(8,128)(2,1)S(1)} %pad_maximum_fusion.1.own_ref, ...), custom_call_target="tpu_custom_call" | custom-call | flops 2000000000 | bytes 4000000 | tf_op jit(solution)/shard_map/attend/pallas_call | solution.py:279
  33.1 14.5 %all_to_all.15 = bf16[32,40,128]{2,1,0:T(8,128)(2,1)S(1)} all-to-all(bf16[32,40,128]{2,1,0:T(8,128)(2,1)S(1)} %bitcast.14), channel_id=1, replica_groups=mesh['y_lo'=2,'z_hi'=4,'z_lo'=2,'y_hi'=4,'x'=4,'core'=2] {'y_lo','z_lo',..., dimensions={0} | all-to-all | bytes 655360 | tf_op jit(solution)/shard_map/all_to_all | solution.py:352
  47.6 0.1 reduce_sum.24
  47.6 0.7 broadcast_in_dim.19
  48.3 6.3 %all-to-all-start.1 = ((bf16[16,40,128]{2,1,0:T(8,128)(2,1)}), bf16[16,40,128]{2,1,0:T(8,128)(2,1)S(1)}, u32[]{:S(2)}, u32[]{:S(2)}) async-start(bf16[16,40,128]{2,1,0:T(8,128)(2,1)} %broadcast_in_dim.19), calls=%async_computation.1 | async-start | bytes 327680 | tf_op jit(solution)/shard_map/all_to_all | solution.py:352
  54.6 0.6 results.1
  55.2 0.0 copy-start.5
  55.2 0.0 copy-start.6
  55.3 2.7 %collective-permute-start.3 = (bf16[6,6,384]{2,1,0:T(8,128)(2,1)S(1)}, bf16[6,6,384]{2,1,0:T(8,128)(2,1)S(1)}, u32[]{:S(2)}, u32[]{:S(2)}) collective-permute-start(bf16[6,6,384]{2,1,0:T(8,128)(2,1)S(1)} %slice.39), channel_id=1, source_target_pairs={{0,1},{1,2},{2,3},{3,4},{4,5},{5,6},{6,7},{7,8},{8,9},{9,10},{10,1... | collective-permute-start | bytes 82952 | tf_op jit(solution)/shard_map/ppermute | solution.py:348
  58.1 8.0 %all-to-all-done.1 = bf16[16,40,128]{2,1,0:T(8,128)(2,1)S(1)} async-done(((bf16[16,40,128]{2,1,0:T(8,128)(2,1)}), bf16[16,40,128]{2,1,0:T(8,128)(2,1)S(1)}, u32[]{:S(2)}, u32[]{:S(2)}) %all-to-all-start.1) | async-done | bytes 163872 | tf_op jit(solution)/shard_map/all_to_all | solution.py:352
  66.1 0.8 broadcast_in_dim.20
  66.9 5.3 %all-to-all-start.2 = ((bf16[32,40,128]{2,1,0:T(8,128)(2,1)}), bf16[32,40,128]{2,1,0:T(8,128)(2,1)S(1)}, u32[]{:S(2)}, u32[]{:S(2)}) async-start(bf16[32,40,128]{2,1,0:T(8,128)(2,1)} %broadcast_in_dim.20), calls=%async_computation.2 | async-start | bytes 655360 | tf_op jit(solution)/shard_map/all_to_all | solution.py:352
  72.1 0.0 collective-permute-done.3
  72.2 0.1 fusion.4
  72.2 3.3 %collective-permute-start.4 = (bf16[3,84,384]{2,1,0:T(8,128)(2,1)S(1)}, bf16[3,84,384]{2,1,0:T(8,128)(2,1)S(1)}, u32[]{:S(2)}, u32[]{:S(2)}) collective-permute-start(bf16[3,84,384]{2,1,0:T(8,128)(2,1)S(1)} %fusion.4), channel_id=1, source_target_pairs={{0,32},{32,64},{64,96},{96,128},{128,160},{160,192},{192,224},{224... | collective-permute-start | bytes 580616 | tf_op jit(solution)/shard_map/ppermute | solution.py:348
  75.5 8.5 %collective-permute-done.4 = bf16[3,84,384]{2,1,0:T(8,128)(2,1)S(1)} collective-permute-done((bf16[3,84,384]{2,1,0:T(8,128)(2,1)S(1)}, bf16[3,84,384]{2,1,0:T(8,128)(2,1)S(1)}, u32[]{:S(2)}, u32[]{:S(2)}) %collective-permute-start.4) | collective-permute-done | bytes 193568 | tf_op jit(solution)/shard_map/ppermute | solution.py:348
  84.0 0.1 fusion.3
  84.1 1.0 %fusion = (bf16[6,84,192]{2,1,0:T(8,128)(2,1)}, bf16[6,84,192]{2,1,0:T(8,128)(2,1)}) fusion(f32[6,84,384]{2,1,0:T(8,128)S(1)} %fusion.3, bf16[6,84,192]{2,1,0:T(8,128)(2,1)S(1)} %copy-done.5, bf16[6,84,192]{2,1,0:T(8,128)(2,1)S(1)} %copy-done.6), kind=kLoop, calls=%fused_computation.1 | loop fusion | flops 580608 | bytes 1548288 | tf_op jit(solution)/shard_map/convert_element_type | solution.py:397
  85.1 0.0 all-to-all-done.2
  85.1 1.1 %finish.1 = (f32[192,576]{1,0:T(8,128)}, f32[192,192]{1,0:T(8,128)}, f32[48,253]{1,0:T(8,128)}, f32[1,192]{1,0:T(1,128)}) custom-call(bf16[1280,128]{1,0:T(8,128)(2,1)S(1)} %bitcast.13), custom_call_target="tpu_custom_call" | custom-call | flops 1000000 | bytes 1000000 | tf_op jit(solution)/shard_map/finish/pallas_call | solution.py:330
  (14 shorter events, 0.1 us)
Async XLA Ops:
  0.6 22.4 %copy-start = (s32[16,224]{1,0:T(8,128)S(1)}, s32[16,224]{1,0:T(8,128)}, u32[]{:S(2)}) copy-start(s32[16,224]{1,0:T(8,128)} %param.12) | copy-start | bytes 43012
  0.6 24.9 %copy-start.1 = (bf16[192,192]{1,0:T(8,128)(2,1)S(1)}, bf16[192,192]{1,0:T(8,128)(2,1)}, u32[]{:S(2)}) copy-start(bf16[192,192]{1,0:T(8,128)(2,1)} %wproj_ref.3) | copy-start | bytes 221188
  0.7 24.9 %copy-start.4 = (bf16[192,576]{1,0:T(8,128)(2,1)S(1)}, bf16[192,576]{1,0:T(8,128)(2,1)}, u32[]{:S(2)}) copy-start(bf16[192,576]{1,0:T(8,128)(2,1)} %wqkv_ref.1) | copy-start | bytes 663556
  0.7 24.9 %copy-start.3 = (f32[192]{0:T(256)S(1)}, f32[192]{0:T(256)}, u32[]{:S(2)}) copy-start(f32[192]{0:T(256)} %param.8) | copy-start | bytes 2308
  2.0 23.6 %collective-permute-start = (bf16[3,84,384]{2,1,0:T(8,128)(2,1)S(1)}, bf16[3,84,384]{2,1,0:T(8,128)(2,1)S(1)}, u32[]{:S(2)}, u32[]{:S(2)}) collective-permute-start(bf16[3,84,384]{2,1,0:T(8,128)(2,1)S(1)} %slice.36), channel_id=1, source_target_pairs={{0,480},{32,0},{64,32},{96,64},{128,96},{160,128},{192,160},{224,1... | collective-permute-start | bytes 580616 | tf_op jit(solution)/shard_map/ppermute | solution.py:348
  14.5 11.1 %collective-permute-start.2 = (bf16[3,6,384]{2,1,0:T(8,128)(2,1)S(1)}, bf16[3,6,384]{2,1,0:T(8,128)(2,1)S(1)}, u32[]{:S(2)}, u32[]{:S(2)}) collective-permute-start(bf16[3,6,384]{2,1,0:T(8,128)(2,1)S(1)} %get-tuple-element.26), channel_id=1, source_target_pairs={{0,511},{1,480},{2,481},{3,482},{4,483},{5,484},{6,485},{7,486},{8... | collective-permute-start | bytes 41480 | tf_op jit(solution)/shard_map/ppermute | solution.py:382
  17.5 8.1 %collective-permute-start.1 = (bf16[3,6,384]{2,1,0:T(8,128)(2,1)S(1)}, bf16[3,6,384]{2,1,0:T(8,128)(2,1)S(1)}, u32[]{:S(2)}, u32[]{:S(2)}) collective-permute-start(bf16[3,6,384]{2,1,0:T(8,128)(2,1)S(1)} %get-tuple-element.27), channel_id=1, source_target_pairs={{0,31},{1,0},{2,1},{3,2},{4,3},{5,4},{6,5},{7,6},{8,7},{9,8},{10,9... | collective-permute-start | bytes 41480 | tf_op jit(solution)/shard_map/ppermute | solution.py:348
  23.2 0.8 copy-start.2
  48.3 17.7 %all-to-all-start.1 = ((bf16[16,40,128]{2,1,0:T(8,128)(2,1)}), bf16[16,40,128]{2,1,0:T(8,128)(2,1)S(1)}, u32[]{:S(2)}, u32[]{:S(2)}) async-start(bf16[16,40,128]{2,1,0:T(8,128)(2,1)} %broadcast_in_dim.19), calls=%async_computation.1 | async-start | bytes 327680 | tf_op jit(solution)/shard_map/all_to_all | solution.py:352
  55.2 28.9 %copy-start.5 = (bf16[6,84,192]{2,1,0:T(8,128)(2,1)S(1)}, bf16[6,84,192]{2,1,0:T(8,128)(2,1)}, u32[]{:S(2)}) copy-start(bf16[6,84,192]{2,1,0:T(8,128)(2,1)} %param.13) | copy-start | bytes 580612
  55.2 28.9 %copy-start.6 = (bf16[6,84,192]{2,1,0:T(8,128)(2,1)S(1)}, bf16[6,84,192]{2,1,0:T(8,128)(2,1)}, u32[]{:S(2)}) copy-start(bf16[6,84,192]{2,1,0:T(8,128)(2,1)} %param.7) | copy-start | bytes 580612
  55.3 16.9 %collective-permute-start.3 = (bf16[6,6,384]{2,1,0:T(8,128)(2,1)S(1)}, bf16[6,6,384]{2,1,0:T(8,128)(2,1)S(1)}, u32[]{:S(2)}, u32[]{:S(2)}) collective-permute-start(bf16[6,6,384]{2,1,0:T(8,128)(2,1)S(1)} %slice.39), channel_id=1, source_target_pairs={{0,1},{1,2},{2,3},{3,4},{4,5},{5,6},{6,7},{7,8},{8,9},{9,10},{10,1... | collective-permute-start | bytes 82952 | tf_op jit(solution)/shard_map/ppermute | solution.py:348
  66.9 18.3 %all-to-all-start.2 = ((bf16[32,40,128]{2,1,0:T(8,128)(2,1)}), bf16[32,40,128]{2,1,0:T(8,128)(2,1)S(1)}, u32[]{:S(2)}, u32[]{:S(2)}) async-start(bf16[32,40,128]{2,1,0:T(8,128)(2,1)} %broadcast_in_dim.20), calls=%async_computation.2 | async-start | bytes 655360 | tf_op jit(solution)/shard_map/all_to_all | solution.py:352
  72.2 11.8 %collective-permute-start.4 = (bf16[3,84,384]{2,1,0:T(8,128)(2,1)S(1)}, bf16[3,84,384]{2,1,0:T(8,128)(2,1)S(1)}, u32[]{:S(2)}, u32[]{:S(2)}) collective-permute-start(bf16[3,84,384]{2,1,0:T(8,128)(2,1)S(1)} %fusion.4), channel_id=1, source_target_pairs={{0,32},{32,64},{64,96},{96,128},{128,160},{160,192},{192,224},{224... | collective-permute-start | bytes 580616 | tf_op jit(solution)/shard_map/ppermute | solution.py:348
